TPU v7x, 32 devices: a whole 2x2x4 slice. The times are simulated.
32 devices in a mesh: morton: 16 (over z, y, x), dp: 2 (over core).
Axes of the slice: x: 2, y: 2, z: 4, core: 2. Of those that a mesh axis runs over, the one named last changes fastest.
Arguments:
- node_feat: bfloat16 [2, 8192, 128], P('dp', 'morton'), may hold values from -6 to 6
- edge_feat: bfloat16 [2, 32768, 128], P('dp', 'morton'), may hold values from -6 to 6
- cot_node: bfloat16 [2, 8192, 128], P('dp', 'morton'), may hold values from -6 to 6
- cot_edge: bfloat16 [2, 32768, 128], P('dp', 'morton'), may hold values from -6 to 6
- senders: int32 [2, 32768], P('dp', 'morton'), may hold values from 0 to 767, as said below
- receivers: int32 [2, 32768], P('dp', 'morton'), may hold values from 0 to 511
- send_rows: int32 [2, 4096], P('dp', 'morton'), may hold values from 0 to 511
- edge_count: int32 [2, 16], P('dp', 'morton'), may hold values from 512 to 2048, as said below
- edge_w1: float32 [384, 128], replicated, may hold values from -0.3125 to 0.3125
- edge_w2: float32 [128, 128], replicated, may hold values from -0.5 to 0.5
- edge_gain: float32 [128], replicated, may hold values from 0.25 to 1.75
- node_w1: float32 [256, 128], replicated, may hold values from -0.375 to 0.375
- node_w2: float32 [128, 128], replicated, may hold values from -0.5 to 0.5
- node_gain: float32 [128], replicated, may hold values from 0.25 to 1.75
Outputs:
- grad_node: float32 [2, 8192, 128], P('dp', 'morton')
- grad_edge: float32 [2, 32768, 128], P('dp', 'morton')
- grad_edge_w1: float32 [384, 128], replicated
- grad_edge_w2: float32 [128, 128], replicated
- grad_edge_gain: float32 [128], replicated
- grad_node_w1: float32 [256, 128], replicated
- grad_node_w2: float32 [128, 128], replicated
- grad_node_gain: float32 [128], replicated
Inputs may be any that keep to these rules, and one draw needn't show every extreme that they name: `senders`: on device m, an entry below 512 is one of its own cells; an entry 512 + k * 64 + q is ghost row q of group k, which comes from device m - d_k with d = (-16/2, -1, +1, +16/2); that device always exists. `send_rows`: entry k * 64 + q of device m is its local cell sent to device m + d_k, with d = (-16/2, -1, +1, +16/2). `edge_count`: edge slots at or beyond the count are empty; some device of every block is full.
All inputs are finite; a program needn't handle non-finite values.
Results may differ from a plain program's by a relative error of at most 0.014.
Values may be sent and summed in bfloat16 or wider, within the bound.
No kernel may reach another device: no remote copies, remote signals or barrier semaphores. Data moves between devices by JAX's collectives and lax.ppermute only.
A program may use at most 64 MiB of HBM per device.

v0:
```python
import jax
import jax.numpy as jnp
from jax import lax
from jax.sharding import PartitionSpec as P


def layer_norm(values, gain):
    center = values - jnp.mean(values, axis=-1, keepdims=True)
    spread = jnp.mean(center * center, axis=-1, keepdims=True)
    return center * lax.rsqrt(spread + 1e-05) * gain


def local_forward(
    cells, ghosts, edges, ew1, ew2, egain, nw1, nw2, ngain, sending, receiving, count
):
    table = jnp.concatenate([cells, ghosts], axis=0)
    joined = jnp.concatenate(
        [
            edges.astype(jnp.bfloat16),
            table[sending].astype(jnp.bfloat16),
            cells[receiving].astype(jnp.bfloat16),
        ],
        axis=1,
    )
    first = jnp.dot(joined, ew1.astype(jnp.bfloat16), preferred_element_type=jnp.float32)
    second = jnp.dot(
        jax.nn.silu(first).astype(jnp.bfloat16),
        ew2.astype(jnp.bfloat16),
        preferred_element_type=jnp.float32,
    )
    live = (jnp.arange(edges.shape[0]) < count).astype(edges.dtype)[:, None]
    edge_new = edges + live * layer_norm(second, egain)
    message = (live * edge_new).astype(jnp.bfloat16)
    gathered = jax.ops.segment_sum(
        message.astype(edges.dtype), receiving, num_segments=cells.shape[0]
    )
    stacked = jnp.concatenate([cells.astype(jnp.bfloat16), gathered.astype(jnp.bfloat16)], axis=1)
    hidden = jnp.dot(stacked, nw1.astype(jnp.bfloat16), preferred_element_type=jnp.float32)
    output = jnp.dot(
        jax.nn.silu(hidden).astype(jnp.bfloat16),
        nw2.astype(jnp.bfloat16),
        preferred_element_type=jnp.float32,
    )
    return (cells + layer_norm(output, ngain), edge_new)


def on_device(
    node_feat,
    edge_feat,
    cot_node,
    cot_edge,
    senders,
    receivers,
    send_rows,
    edge_count,
    edge_w1,
    edge_w2,
    edge_gain,
    node_w1,
    node_w2,
    node_gain,
):
    peers = lax.axis_size("morton")
    rank = lax.axis_index("morton")
    offsets = (-(peers // 2), -1, 1, peers // 2)
    width = node_feat.shape[2]
    quota = send_rows.shape[1] // 4
    outgoing = send_rows[0].reshape(4, quota)
    cells_bf = node_feat[0]
    picked = [cells_bf[outgoing[k]] for k in range(4)]
    arrived = []
    buffer = jnp.zeros((peers, quota, width), jnp.bfloat16)
    for k in range(4):
        target = jax.nn.one_hot(rank + offsets[k], peers, dtype=jnp.bfloat16)
        buffer = buffer + target[:, None, None] * picked[k][None]
    received = lax.all_to_all(buffer, "morton", split_axis=0, concat_axis=0, tiled=True)
    for k in range(4):
        source = rank - offsets[k]
        valid = ((source >= 0) & (source < peers)).astype(jnp.float32)
        arrived.append(received[jnp.clip(source, 0, peers - 1)].astype(jnp.float32) * valid)
    ghosts = jnp.concatenate(arrived, axis=0)
    cells = cells_bf.astype(jnp.float32)
    edges = edge_feat[0].astype(jnp.float32)
    sending = senders[0]
    receiving = receivers[0]
    count = edge_count[0, 0]

    def forward(cells, ghosts, edges, ew1, ew2, egain, nw1, nw2, ngain):
        return local_forward(
            cells, ghosts, edges, ew1, ew2, egain, nw1, nw2, ngain, sending, receiving, count
        )

    outputs, pullback = jax.vjp(
        forward, cells, ghosts, edges, edge_w1, edge_w2, edge_gain, node_w1, node_w2, node_gain
    )
    grads = pullback((cot_node[0].astype(jnp.float32), cot_edge[0].astype(jnp.float32)))
    grad_cells = grads[0]
    ghost_grads = grads[1].reshape(4, quota, width)
    buffer = jnp.zeros((peers, quota, width), jnp.float32)
    for k in range(4):
        target = jax.nn.one_hot(rank - offsets[k], peers, dtype=jnp.float32)
        buffer = buffer + target[:, None, None] * ghost_grads[k][None]
    returned = lax.all_to_all(
        buffer.astype(jnp.bfloat16), "morton", split_axis=0, concat_axis=0, tiled=True
    ).astype(buffer.dtype)
    for k in range(4):
        reader = rank + offsets[k]
        valid = ((reader >= 0) & (reader < peers)).astype(jnp.float32)
        grad_cells = grad_cells.at[outgoing[k]].add(
            returned[jnp.clip(reader, 0, peers - 1)] * valid
        )
    summed = lax.psum(
        (grads[3], grads[4], grads[5], grads[6], grads[7], grads[8]), ("morton", "dp")
    )
    factor = 1.0 / jnp.sqrt(jnp.float32(lax.axis_size("dp") * peers * edge_feat.shape[1]))
    return (
        grad_cells[None],
        grads[2][None],
        summed[0] * factor,
        summed[1] * factor,
        summed[2] * factor,
        summed[3] * factor,
        summed[4] * factor,
        summed[5] * factor,
    )


def solution(mesh):
    in_specs = (
        P("dp", "morton", None),
        P("dp", "morton", None),
        P("dp", "morton", None),
        P("dp", "morton", None),
        P("dp", "morton"),
        P("dp", "morton"),
        P("dp", "morton"),
        P("dp", "morton"),
        P(),
        P(),
        P(),
        P(),
        P(),
        P(),
    )
    out_specs = (P("dp", "morton", None), P("dp", "morton", None), P(), P(), P(), P(), P(), P())
    return jax.shard_map(
        on_device, mesh=mesh, in_specs=in_specs, out_specs=out_specs, check_vma=False
    )
```

profile of v0, /device:TPU:1, one launch (start us, length us, event | category | flops | bytes accessed | tf_op | source)
XLA Modules:
  0.0 282.5 jit_solution(1534379466530907861)
XLA Ops:
  8.6 1.5 gather_fusion.3
  10.2 1.5 gather_fusion.1
  11.7 1.5 gather_fusion.2
  13.2 1.5 gather_fusion
  15.6 7.5 %all-to-all-start = ((bf16[16,64,128]{2,1,0:T(8,128)(2,1)}), bf16[16,64,128]{2,1,0:T(8,128)(2,1)S(1)}, u32[]{:S(2)}, u32[]{:S(2)}) async-start(bf16[16,64,128]{2,1,0:T(8,128)(2,1)} %multiply_add_fusion), calls=%async_computation | async-start | bytes 524288 | tf_op jit(solution)/shard_map/all_to_all | solution.py:76
  23.7 1.3 and_reduce_fusion
  29.0 6.2 %gather_fusion.5 = bf16[2048,128]{1,0:T(8,128)(2,1)S(1)} fusion(bf16[512,128]{1,0:T(8,128)(2,1)S(1)} %bitcast.84, s32[2048]{0:T(1024)S(1)} %get-tuple-element.56), kind=kCustom, calls=%fused_computation.5 | custom fusion | bytes 1056768 | tf_op jit(solution)/shard_map/jvp()/gather | solution.py:21
  35.5 6.2 %gather_fusion.4 = bf16[2048,128]{1,0:T(8,128)(2,1)S(1)} fusion(bf16[768,128]{1,0:T(8,128)(2,1)S(1)} %bitcast_dynamic-update-slice_fusion, s32[2048]{0:T(1024)S(1)} %broadcast_clamp_fusion.2), kind=kCustom, calls=%fused_computation.4 | custom fusion | bytes 1056768 | tf_op jit(solution)/shard_map/jvp()/gather | solution.py:20
  45.5 1.3 copy.45
  46.8 12.1 %scatter_custom_fusion = f32[512,128]{1,0:T(8,128)S(1)} fusion(s32[2048]{0:T(1024)} %bitcast.91, f32[2048,128]{1,0:T(8,128)} %copy.45, f32[]{:T(128)} %constant.24.clone.1), kind=kCustom, calls=%fused_computation.77 | custom fusion | flops 262144 | bytes 262656 | tf_op jit(solution)/shard_map/jvp()/scatter-add | solution.py:34
  59.2 1.2 fusion.76
  61.2 0.9 fusion.5
  64.5 6.2 %gather_fusion.6 = bf16[2048,128]{1,0:T(8,128)(2,1)S(1)} fusion(bf16[512,128]{1,0:T(8,128)(2,1)S(1)} %copy.48, s32[2048]{0:T(1024)S(1)} %copy-done.21), kind=kCustom, calls=%fused_computation.6 | custom fusion | bytes 1056768 | tf_op jit(solution)/shard_map/transpose(jvp())/gather | solution.py:34
  72.9 1.1 fusion.4
  75.2 1.2 fusion.2
  76.4 1.5 convolution_convert_fusion
  78.4 1.3 copy.51
  79.8 12.0 %scatter_custom_fusion.1 = f32[768,128]{1,0:T(8,128)S(1)} fusion(s32[2048]{0:T(1024)} %bitcast.94, f32[2048,128]{1,0:T(8,128)} %copy.51, f32[]{:T(128)} %constant.24.clone.1), kind=kCustom, calls=%fused_computation.71 | custom fusion | flops 262144 | bytes 393728 | tf_op jit(solution)/shard_map/transpose(jvp())/scatter-add | solution.py:20
  92.7 40.0 %all-reduce = (f32[128]{0:T(128)S(1)}, f32[128]{0:T(128)S(1)}) all-reduce(f32[128]{0:T(128)S(1)} %get-tuple-element.24, f32[128]{0:T(128)S(1)} %copy-done.35), channel_id=1, replica_groups=mesh['morton'=16,'dp'=2] {'morton','dp'}, use_global_device_ids=true, to_apply=%region_18.19 | all-reduce | flops 256 | bytes 2048 | tf_op jit(solution)/shard_map/psum | solution.py:112
  132.8 0.9 add_convert_fusion
  134.2 1.3 copy.55
  136.6 5.2 %all-to-all-start.1 = ((bf16[16,64,128]{2,1,0:T(8,128)(2,1)}), bf16[16,64,128]{2,1,0:T(8,128)(2,1)S(1)}, u32[]{:S(2)}, u32[]{:S(2)}) async-start(bf16[16,64,128]{2,1,0:T(8,128)(2,1)} %add_convert_fusion), calls=%async_computation.1 | async-start | bytes 524288 | tf_op jit(solution)/shard_map/all_to_all | solution.py:103
  141.8 11.6 %scatter_fusion = f32[512,128]{1,0:T(8,128)S(1)} fusion(f32[512,128]{1,0:T(8,128)S(1)} %copy.53, s32[2048]{0:T(1024)S(1)} %bitcast.90, f32[2048,128]{1,0:T(8,128)S(1)} %copy.54), kind=kCustom, calls=%fused_computation.9 | custom fusion | flops 262144 | bytes 3153920 | tf_op jit(solution)/shard_map/transpose(jvp())/scatter-add | solution.py:21
  153.9 110.2 %all-reduce.4.cloned.1.call-done = (f32[384,128]{1,0:T(8,128)}, f32[128,128]{1,0:T(8,128)}, f32[256,128]{1,0:T(8,128)}, f32[128,128]{1,0:T(8,128)}) async-done(((f32[384,128]{1,0:T(8,128)}, f32[128,128]{1,0:T(8,128)}, f32[256,128]{1,0:T(8,128)}, f32[128,128]{1,0:T(8,128)}), (f32[384,128]{1,0:T(8,128)}, f32[128,128]{1,0:T(8,128)}, f32[256,128]{1,0:T(8,128)}, ...) | async-done | bytes 458768 | tf_op jit(solution)/shard_map/psum | solution.py:112
  264.1 1.5 broadcast_multiply_fusion.3
  265.5 1.5 broadcast_multiply_fusion.2
  267.0 1.6 broadcast_multiply_fusion.1
  268.6 1.6 broadcast_multiply_fusion
  270.2 1.2 scatter_custom_fusion.3
  271.4 1.2 scatter_custom_fusion.4
  272.6 1.2 scatter_custom_fusion.5
  273.7 1.2 scatter_custom_fusion.6
  (144 shorter events, 21.0 us)
Async XLA Ops:
  7.2 20.0 %copy-start.20 = (s32[1,2048]{1,0:T(1,128)S(1)}, s32[1,2048]{1,0:T(1,128)}, u32[]{:S(2)}) copy-start(s32[1,2048]{1,0:T(1,128)} %param.19) | copy-start | bytes 24580
  7.2 21.2 %copy-start.15 = (bf16[1,512,128]{2,1,0:T(8,128)(2,1)S(1)}, bf16[1,512,128]{2,1,0:T(8,128)(2,1)}, u32[]{:S(2)}) copy-start(bf16[1,512,128]{2,1,0:T(8,128)(2,1)} %param.16) | copy-start | bytes 393220
  7.2 21.3 %copy-start.5 = (bf16[1,2048,128]{2,1,0:T(8,128)(2,1)S(1)}, bf16[1,2048,128]{2,1,0:T(8,128)(2,1)}, u32[]{:S(2)}) copy-start(bf16[1,2048,128]{2,1,0:T(8,128)(2,1)} %param.17) | copy-start | bytes 1572868
  7.2 21.5 %copy-start.6 = (bf16[1,2048,128]{2,1,0:T(8,128)(2,1)S(1)}, bf16[1,2048,128]{2,1,0:T(8,128)(2,1)}, u32[]{:S(2)}) copy-start(bf16[1,2048,128]{2,1,0:T(8,128)(2,1)} %param.15) | copy-start | bytes 1572868
  8.1 3.6 %copy-start.31 = (s32[64]{0:T(128)}, s32[64]{0:T(128)S(1)}, u32[]{:S(2)}) copy-start(s32[64]{0:T(128)S(1)} %get-tuple-element.49) | copy-start | bytes 772
  8.1 3.6 %copy-start.32 = (s32[64]{0:T(128)}, s32[64]{0:T(128)S(1)}, u32[]{:S(2)}) copy-start(s32[64]{0:T(128)S(1)} %get-tuple-element.50) | copy-start | bytes 772
  15.6 13.3 %copy-start.1 = (bf16[1,512,128]{2,1,0:T(8,128)(2,1)S(1)}, bf16[1,512,128]{2,1,0:T(8,128)(2,1)}, u32[]{:S(2)}) copy-start(bf16[1,512,128]{2,1,0:T(8,128)(2,1)} %param.14) | copy-start | bytes 393220
  15.6 19.8 %all-to-all-start = ((bf16[16,64,128]{2,1,0:T(8,128)(2,1)}), bf16[16,64,128]{2,1,0:T(8,128)(2,1)S(1)}, u32[]{:S(2)}, u32[]{:S(2)}) async-start(bf16[16,64,128]{2,1,0:T(8,128)(2,1)} %multiply_add_fusion), calls=%async_computation | async-start | bytes 524288 | tf_op jit(solution)/shard_map/all_to_all | solution.py:76
  23.2 240.9 %all-reduce.4.cloned.1.call-start = ((), (), s32[]{:S(2)}) async-start(), calls=%async_computation.2 | async-start | bytes 917504 | tf_op jit(solution)/shard_map/psum | solution.py:112
  25.8 2.6 copy-start.18
  27.1 8.2 %copy-start.22 = (s32[2048,1]{0,1:T(1,128)}, s32[2048,1]{0,1:T(1,128)S(1)}, u32[]{:S(2)}) copy-start(s32[2048,1]{0,1:T(1,128)S(1)} %compare_select_fusion.1) | copy-start | bytes 24580
  35.4 6.6 %copy-start.7 = (bf16[2048,128]{0,1:T(8,128)(2,1)}, bf16[2048,128]{0,1:T(8,128)(2,1)S(1)}, u32[]{:S(2)}) copy-start(bf16[2048,128]{0,1:T(8,128)(2,1)S(1)} %copy.44) | copy-start | bytes 1572868
  35.5 6.4 %copy-start.12 = (f32[384,128]{1,0:T(8,128)S(1)}, f32[384,128]{1,0:T(8,128)}, u32[]{:S(2)}) copy-start(f32[384,128]{1,0:T(8,128)} %param.22) | copy-start | bytes 589828
  42.9 2.3 copy-start.24
  45.5 13.4 %copy-start.11 = (f32[256,128]{1,0:T(8,128)S(1)}, f32[256,128]{1,0:T(8,128)}, u32[]{:S(2)}) copy-start(f32[256,128]{1,0:T(8,128)} %param.25) | copy-start | bytes 393220
  46.8 13.5 %copy-start.26 = (f32[128]{0:T(128)S(1)}, f32[128]{0:T(128)}, u32[]{:S(2)}) copy-start(f32[128]{0:T(128)} %param.27) | copy-start | bytes 1540
  59.2 2.9 %copy-start.36 = (f32[128,128]{1,0:T(8,128)S(1)}, f32[128,128]{1,0:T(8,128)}, u32[]{:S(2)}) copy-start(f32[128,128]{1,0:T(8,128)} %param.26) | copy-start | bytes 196612
  62.1 2.3 copy-start.21
  64.4 6.4 %copy-start.14 = (f32[2048]{0:T(1024)S(1)}, f32[2048]{0:T(1024)}, u32[]{:S(2)}) copy-start(f32[2048]{0:T(1024)} %copy-done.13) | copy-start | bytes 24580
  64.5 6.4 %copy-start.23 = (pred[2048]{0:T(1024)(128)(4,1)S(1)}, pred[2048]{0:T(1024)(128)(4,1)}, u32[]{:S(2)}) copy-start(pred[2048]{0:T(1024)(128)(4,1)} %and_reduce_fusion) | copy-start | bytes 6148
  64.5 6.4 %copy-start.25 = (f32[128]{0:T(128)S(1)}, f32[128]{0:T(128)}, u32[]{:S(2)}) copy-start(f32[128]{0:T(128)} %param.24) | copy-start | bytes 1540
  71.6 1.2 copy-start.40
  72.9 1.1 copy-start.38
  74.0 1.2 copy-start.10
  79.7 12.2 %copy-start.4 = (bf16[512,256]{0,1:T(8,128)(2,1)S(1)}, bf16[512,256]{0,1:T(8,128)(2,1)}, u32[]{:S(2)}) copy-start(bf16[512,256]{0,1:T(8,128)(2,1)} %copy-done.3) | copy-start | bytes 786436
  79.7 13.0 %copy-start.35 = (f32[128]{0:T(128)S(1)}, f32[128]{0:T(128)}, u32[]{:S(2)}) copy-start(f32[128]{0:T(128)} %get-tuple-element.26) | copy-start | bytes 1540
  79.7 53.0 %copy-start.27 = (f32[16]{0:T(128)S(1)}, f32[16]{0:T(128)}, u32[]{:S(2)}) copy-start(f32[16]{0:T(128)} %get-tuple-element.67) | copy-start | bytes 196
  79.7 53.0 %copy-start.28 = (f32[16]{0:T(128)S(1)}, f32[16]{0:T(128)}, u32[]{:S(2)}) copy-start(f32[16]{0:T(128)} %get-tuple-element.68) | copy-start | bytes 196
  79.7 53.0 %copy-start.29 = (f32[16]{0:T(128)S(1)}, f32[16]{0:T(128)}, u32[]{:S(2)}) copy-start(f32[16]{0:T(128)} %get-tuple-element.65) | copy-start | bytes 196
  79.7 53.0 %copy-start.30 = (f32[16]{0:T(128)S(1)}, f32[16]{0:T(128)}, u32[]{:S(2)}) copy-start(f32[16]{0:T(128)} %get-tuple-element.66) | copy-start | bytes 196
  135.5 6.2 %copy-start.19 = (s32[2048,1]{0,1:T(1,128)S(1)}, s32[2048,1]{0,1:T(1,128)}, u32[]{:S(2)}) copy-start(s32[2048,1]{0,1:T(1,128)} %copy-done.18) | copy-start | bytes 24580
  136.6 133.6 %all-to-all-start.1 = ((bf16[16,64,128]{2,1,0:T(8,128)(2,1)}), bf16[16,64,128]{2,1,0:T(8,128)(2,1)S(1)}, u32[]{:S(2)}, u32[]{:S(2)}) async-start(bf16[16,64,128]{2,1,0:T(8,128)(2,1)} %add_convert_fusion), calls=%async_computation.1 | async-start | bytes 524288 | tf_op jit(solution)/shard_map/all_to_all | solution.py:103
  (12 other events, 9.0 us)
Sparse Core Ops, SparseCore 0:
  132.9 131.1 all-reduce.3
where the time goes:
time: 284 us; the launch traced here: 282 us
  waiting for transfers between devices  110 us (39%)
  other arithmetic  58.2 us (20%)
  blocking collectives  40 us (14%)
  local copies, waits for them, and re-layouts  36.5 us (13%)
  between operations  15.4 us (5%)
  starting transfers between devices  12.7 us (4%)
  matrix products  9.35 us (3%)
    psum x1, waiting for transfers between devices, on_device(): lax.psum((grads[3], grads[4], grads[5], grads[6], grads[7], grads[8]), ('...  110 us
    psum x1, blocking collectives, on_device(): lax.psum((grads[3], grads[4], grads[5], grads[6], grads[7], grads[8]), ('...  40 us
    scatter-add x1, other arithmetic, local_forward(): jax.ops.segment_sum(message.astype(edges.dtype), receiving, num_segments=...  12.1 us
    scatter-add x1, other arithmetic, local_forward(): table[sending].astype(jnp.bfloat16)  12 us
    scatter-add x1, other arithmetic, local_forward(): cells[receiving].astype(jnp.bfloat16)  11.6 us
    unnamed x87, local copies, waits for them, and re-layouts  8.03 us
    all_to_all x1, starting transfers between devices, on_device(): lax.all_to_all(buffer, 'morton', split_axis=0, concat_axis=0, tiled=True)  7.53 us
    gather x2, local copies, waits for them, and re-layouts, local_forward(): cells[receiving].astype(jnp.bfloat16)  6.4 us
  transfers between devices with their start and end apart: 3, of which 1 were waited for; matrix products, arithmetic and copies ran while one was open for 12% of the time, Pallas kernels for 0%

commit v1 on v0

--- a/solution.py
+++ b/solution.py
@@ -110,7 +110,7 @@
             returned[jnp.clip(reader, 0, peers - 1)] * valid
         )
     summed = lax.psum(
-        (grads[3], grads[4], grads[5], grads[6], grads[7], grads[8]), ("morton", "dp")
+        lax.psum((grads[3], grads[4], grads[5], grads[6], grads[7], grads[8]), "dp"), "morton"
     )
     factor = 1.0 / jnp.sqrt(jnp.float32(lax.axis_size("dp") * peers * edge_feat.shape[1]))
     return (

time: 284 us -> 258 us (0.908)
  waiting for transfers between devices: 110 us -> 81 us
  other arithmetic: 58.2 us -> 61.7 us
    psum x1 -> x2, waiting for transfers between devices: 110 us -> 80.3 us  [the longest x1 57.1 us: on_device(): lax.psum(lax.psum((grads[3], grads[4], grads[5], grads[6], grads[7], grad...]
    psum x1 -> x2, blocking collectives: 40 us -> 37.3 us  [the longest x1 34.9 us: on_device(): lax.psum(lax.psum((grads[3], grads[4], grads[5], grads[6], grads[7], grad...]
    unnamed x87 -> x93, local copies, waits for them, and re-layouts: 8.03 us -> 8.04 us
  transfers between devices with their start and end apart: 3 -> 4, of which waited for: 1 -> 2; matrix products, arithmetic and copies ran while one was open for 12% -> 13% of each run, Pallas kernels for 0% -> 0%
where the time goes in v1:
time: 258 us; the launch traced here: 255 us
  waiting for transfers between devices  81 us (31%)
  other arithmetic  61.7 us (24%)
  blocking collectives  37.3 us (14%)
  local copies, waits for them, and re-layouts  37.2 us (14%)
  between operations  15.4 us (6%)
  starting transfers between devices  14 us (5%)
  matrix products  8.4 us (3%)
    psum x1, waiting for transfers between devices, on_device(): lax.psum(lax.psum((grads[3], grads[4], grads[5], grads[6], grads[7], grad...  57.1 us
    psum x1, blocking collectives, on_device(): lax.psum(lax.psum((grads[3], grads[4], grads[5], grads[6], grads[7], grad...  34.9 us
    psum x1, waiting for transfers between devices, on_device(): lax.psum((grads[3], grads[4], grads[5], grads[6], grads[7], grads[8]), 'dp')  23.2 us
    scatter-add x1, other arithmetic, local_forward(): jax.ops.segment_sum(message.astype(edges.dtype), receiving, num_segments=...  12.1 us
    scatter-add x1, other arithmetic, local_forward(): table[sending].astype(jnp.bfloat16)  12 us
    scatter-add x1, other arithmetic, local_forward(): cells[receiving].astype(jnp.bfloat16)  11.6 us
    unnamed x93, local copies, waits for them, and re-layouts  8.04 us
    all_to_all x1, starting transfers between devices, on_device(): lax.all_to_all(buffer, 'morton', split_axis=0, concat_axis=0, tiled=True)  7.53 us
  transfers between devices with their start and end apart: 4, of which 2 were waited for; matrix products, arithmetic and copies ran while one was open for 13% of the time, Pallas kernels for 0%

profile of v1, /device:TPU:1, one launch (start us, length us, event | category | flops | bytes accessed | tf_op | source)
XLA Modules:
  0.0 255.1 jit_solution(17952820715654709720)
XLA Ops:
  8.7 1.5 gather_fusion.3
  10.2 1.5 gather_fusion.1
  11.8 1.5 gather_fusion.2
  13.3 1.5 gather_fusion
  15.7 7.5 %all-to-all-start = ((bf16[16,64,128]{2,1,0:T(8,128)(2,1)}), bf16[16,64,128]{2,1,0:T(8,128)(2,1)S(1)}, u32[]{:S(2)}, u32[]{:S(2)}) async-start(bf16[16,64,128]{2,1,0:T(8,128)(2,1)} %multiply_add_fusion), calls=%async_computation | async-start | bytes 524288 | tf_op jit(solution)/shard_map/all_to_all | solution.py:76
  23.8 1.3 and_reduce_fusion
  29.0 6.2 %gather_fusion.5 = bf16[2048,128]{1,0:T(8,128)(2,1)S(1)} fusion(bf16[512,128]{1,0:T(8,128)(2,1)S(1)} %bitcast.84, s32[2048]{0:T(1024)S(1)} %get-tuple-element.62), kind=kCustom, calls=%fused_computation.5 | custom fusion | bytes 1056768 | tf_op jit(solution)/shard_map/jvp()/gather | solution.py:21
  35.6 6.2 %gather_fusion.4 = bf16[2048,128]{1,0:T(8,128)(2,1)S(1)} fusion(bf16[768,128]{1,0:T(8,128)(2,1)S(1)} %bitcast_dynamic-update-slice_fusion, s32[2048]{0:T(1024)S(1)} %broadcast_clamp_fusion.2), kind=kCustom, calls=%fused_computation.4 | custom fusion | bytes 1056768 | tf_op jit(solution)/shard_map/jvp()/gather | solution.py:20
  45.6 1.3 copy.45
  46.9 12.1 %scatter_custom_fusion = f32[512,128]{1,0:T(8,128)S(1)} fusion(s32[2048]{0:T(1024)} %bitcast.91, f32[2048,128]{1,0:T(8,128)} %copy.45, f32[]{:T(128)} %constant.24.clone.1), kind=kCustom, calls=%fused_computation.77 | custom fusion | flops 262144 | bytes 262656 | tf_op jit(solution)/shard_map/jvp()/scatter-add | solution.py:34
  64.6 6.2 %gather_fusion.6 = bf16[2048,128]{1,0:T(8,128)(2,1)S(1)} fusion(bf16[512,128]{1,0:T(8,128)(2,1)S(1)} %copy.48, s32[2048]{0:T(1024)S(1)} %copy-done.25), kind=kCustom, calls=%fused_computation.6 | custom fusion | bytes 1056768 | tf_op jit(solution)/shard_map/transpose(jvp())/gather | solution.py:34
  75.8 1.2 fusion.2
  77.7 1.2 slice_convert_fusion
  78.9 1.3 copy.51
  80.2 12.0 %scatter_custom_fusion.1 = f32[768,128]{1,0:T(8,128)S(1)} fusion(s32[2048]{0:T(1024)} %bitcast.94, f32[2048,128]{1,0:T(8,128)} %copy.51, f32[]{:T(128)} %constant.24.clone.1), kind=kCustom, calls=%fused_computation.71 | custom fusion | flops 262144 | bytes 393728 | tf_op jit(solution)/shard_map/transpose(jvp())/scatter-add | solution.py:20
  94.0 1.6 add_convert_fusion
  95.6 6.4 %all-to-all-start.1 = ((bf16[16,64,128]{2,1,0:T(8,128)(2,1)}), bf16[16,64,128]{2,1,0:T(8,128)(2,1)}, u32[]{:S(2)}, u32[]{:S(2)}) async-start(bf16[16,64,128]{2,1,0:T(8,128)(2,1)} %add_convert_fusion), calls=%async_computation.1 | async-start | bytes 524288 | tf_op jit(solution)/shard_map/all_to_all | solution.py:103
  102.8 1.2 add_bitcast_fusion
  104.0 23.2 %all-reduce.9.cloned.1.call-done = (f32[384,128]{1,0:T(8,128)}, f32[128,128]{1,0:T(8,128)}, f32[256,128]{1,0:T(8,128)}, f32[128,128]{1,0:T(8,128)}) async-done(((f32[384,128]{1,0:T(8,128)}, f32[128,128]{1,0:T(8,128)}, f32[256,128]{1,0:T(8,128)}, f32[128,128]{1,0:T(8,128)}), (f32[384,128]{1,0:T(8,128)}, f32[128,128]{1,0:T(8,128)}, f32[256,128]{1,0:T(8,128)}, ...) | async-done | bytes 458768 | tf_op jit(solution)/shard_map/psum | solution.py:113
  127.3 1.3 copy.55
  129.3 11.6 %scatter_fusion = f32[512,128]{1,0:T(8,128)S(1)} fusion(f32[512,128]{1,0:T(8,128)S(1)} %copy.53, s32[2048]{0:T(1024)S(1)} %bitcast.90, f32[2048,128]{1,0:T(8,128)S(1)} %copy.54), kind=kCustom, calls=%fused_computation.9 | custom fusion | flops 262144 | bytes 3153920 | tf_op jit(solution)/shard_map/transpose(jvp())/scatter-add | solution.py:21
  140.9 2.5 all-reduce.2
  143.4 34.9 %all-reduce = (f32[128]{0:T(128)S(1)}, f32[128]{0:T(128)S(1)}) all-reduce(f32[128]{0:T(128)S(1)} %get-tuple-element.36, f32[128]{0:T(128)S(1)} %get-tuple-element.37), channel_id=1, replica_groups=mesh['morton'=16,'dp'=2] {'morton'}, use_global_device_ids=true, to_apply=%region_21.22 | all-reduce | flops 256 | bytes 2048 | tf_op jit(solution)/shard_map/psum | solution.py:112
  180.3 1.2 scatter_custom_fusion.3
  181.5 1.2 scatter_custom_fusion.4
  182.7 1.2 scatter_custom_fusion.5
  183.8 1.2 scatter_custom_fusion.6
  185.0 57.1 %all-reduce.7.cloned.1.call-done = (f32[384,128]{1,0:T(8,128)}, f32[128,128]{1,0:T(8,128)}, f32[256,128]{1,0:T(8,128)}, f32[128,128]{1,0:T(8,128)}) async-done(((f32[384,128]{1,0:T(8,128)}, f32[128,128]{1,0:T(8,128)}, f32[256,128]{1,0:T(8,128)}, f32[128,128]{1,0:T(8,128)}), (f32[384,128]{1,0:T(8,128)}, f32[128,128]{1,0:T(8,128)}, f32[256,128]{1,0:T(8,128)}, ...) | async-done | bytes 458768 | tf_op jit(solution)/shard_map/psum | solution.py:112
  242.1 1.6 broadcast_multiply_fusion
  243.7 1.5 broadcast_multiply_fusion.3
  245.2 1.5 broadcast_multiply_fusion.2
  246.7 1.6 broadcast_multiply_fusion.1
  (154 shorter events, 26.5 us)
Async XLA Ops:
  7.2 20.1 %copy-start.24 = (s32[1,2048]{1,0:T(1,128)S(1)}, s32[1,2048]{1,0:T(1,128)}, u32[]{:S(2)}) copy-start(s32[1,2048]{1,0:T(1,128)} %param.19) | copy-start | bytes 24580
  7.2 21.3 %copy-start.19 = (bf16[1,512,128]{2,1,0:T(8,128)(2,1)S(1)}, bf16[1,512,128]{2,1,0:T(8,128)(2,1)}, u32[]{:S(2)}) copy-start(bf16[1,512,128]{2,1,0:T(8,128)(2,1)} %param.16) | copy-start | bytes 393220
  7.2 21.4 %copy-start.8 = (bf16[1,2048,128]{2,1,0:T(8,128)(2,1)S(1)}, bf16[1,2048,128]{2,1,0:T(8,128)(2,1)}, u32[]{:S(2)}) copy-start(bf16[1,2048,128]{2,1,0:T(8,128)(2,1)} %param.17) | copy-start | bytes 1572868
  7.2 21.6 %copy-start.9 = (bf16[1,2048,128]{2,1,0:T(8,128)(2,1)S(1)}, bf16[1,2048,128]{2,1,0:T(8,128)(2,1)}, u32[]{:S(2)}) copy-start(bf16[1,2048,128]{2,1,0:T(8,128)(2,1)} %param.15) | copy-start | bytes 1572868
  8.1 3.6 %copy-start.33 = (s32[64]{0:T(128)}, s32[64]{0:T(128)S(1)}, u32[]{:S(2)}) copy-start(s32[64]{0:T(128)S(1)} %get-tuple-element.55) | copy-start | bytes 772
  8.1 3.6 %copy-start.34 = (s32[64]{0:T(128)}, s32[64]{0:T(128)S(1)}, u32[]{:S(2)}) copy-start(s32[64]{0:T(128)S(1)} %get-tuple-element.56) | copy-start | bytes 772
  15.7 13.4 %copy-start.1 = (bf16[1,512,128]{2,1,0:T(8,128)(2,1)S(1)}, bf16[1,512,128]{2,1,0:T(8,128)(2,1)}, u32[]{:S(2)}) copy-start(bf16[1,512,128]{2,1,0:T(8,128)(2,1)} %param.14) | copy-start | bytes 393220
  15.7 19.8 %all-to-all-start = ((bf16[16,64,128]{2,1,0:T(8,128)(2,1)}), bf16[16,64,128]{2,1,0:T(8,128)(2,1)S(1)}, u32[]{:S(2)}, u32[]{:S(2)}) async-start(bf16[16,64,128]{2,1,0:T(8,128)(2,1)} %multiply_add_fusion), calls=%async_computation | async-start | bytes 524288 | tf_op jit(solution)/shard_map/all_to_all | solution.py:76
  25.8 2.6 %copy-start.22 = (s32[2048,1]{0,1:T(1,128)}, s32[2048,1]{0,1:T(1,128)S(1)}, u32[]{:S(2)}) copy-start(s32[2048,1]{0,1:T(1,128)S(1)} %compare_select_fusion) | copy-start | bytes 24580
  27.2 8.2 %copy-start.26 = (s32[2048,1]{0,1:T(1,128)}, s32[2048,1]{0,1:T(1,128)S(1)}, u32[]{:S(2)}) copy-start(s32[2048,1]{0,1:T(1,128)S(1)} %compare_select_fusion.1) | copy-start | bytes 24580
  35.4 6.6 %copy-start.10 = (bf16[2048,128]{0,1:T(8,128)(2,1)}, bf16[2048,128]{0,1:T(8,128)(2,1)S(1)}, u32[]{:S(2)}) copy-start(bf16[2048,128]{0,1:T(8,128)(2,1)S(1)} %copy.44) | copy-start | bytes 1572868
  35.6 6.4 %copy-start.15 = (f32[384,128]{1,0:T(8,128)S(1)}, f32[384,128]{1,0:T(8,128)}, u32[]{:S(2)}) copy-start(f32[384,128]{1,0:T(8,128)} %param.22) | copy-start | bytes 589828
  43.0 2.3 copy-start.28
  45.6 13.4 %copy-start.14 = (f32[256,128]{1,0:T(8,128)S(1)}, f32[256,128]{1,0:T(8,128)}, u32[]{:S(2)}) copy-start(f32[256,128]{1,0:T(8,128)} %param.25) | copy-start | bytes 393220
  46.9 13.5 %copy-start.30 = (f32[128]{0:T(128)S(1)}, f32[128]{0:T(128)}, u32[]{:S(2)}) copy-start(f32[128]{0:T(128)} %param.27) | copy-start | bytes 1540
  59.2 2.9 %copy-start.39 = (f32[128,128]{1,0:T(8,128)S(1)}, f32[128,128]{1,0:T(8,128)}, u32[]{:S(2)}) copy-start(f32[128,128]{1,0:T(8,128)} %param.26) | copy-start | bytes 196612
  62.2 2.3 copy-start.25
  64.5 6.4 %copy-start.18 = (f32[2048]{0:T(1024)S(1)}, f32[2048]{0:T(1024)}, u32[]{:S(2)}) copy-start(f32[2048]{0:T(1024)} %copy-done.17) | copy-start | bytes 24580
  64.5 6.4 %copy-start.27 = (pred[2048]{0:T(1024)(128)(4,1)S(1)}, pred[2048]{0:T(1024)(128)(4,1)}, u32[]{:S(2)}) copy-start(pred[2048]{0:T(1024)(128)(4,1)} %and_reduce_fusion) | copy-start | bytes 6148
  64.5 6.4 %copy-start.29 = (f32[128]{0:T(128)S(1)}, f32[128]{0:T(128)}, u32[]{:S(2)}) copy-start(f32[128]{0:T(128)} %param.24) | copy-start | bytes 1540
  72.1 1.4 copy-start.43
  78.9 15.1 %copy-start.31 = (f32[16]{0:T(128)S(1)}, f32[16]{0:T(128)}, u32[]{:S(2)}) copy-start(f32[16]{0:T(128)} %get-tuple-element.73) | copy-start | bytes 196
  78.9 15.1 %copy-start.32 = (f32[16]{0:T(128)S(1)}, f32[16]{0:T(128)}, u32[]{:S(2)}) copy-start(f32[16]{0:T(128)} %get-tuple-element.74) | copy-start | bytes 196
  80.2 22.6 %copy-start.3 = (bf16[2048,128]{0,1:T(8,128)(2,1)S(1)}, bf16[2048,128]{0,1:T(8,128)(2,1)}, u32[]{:S(2)}) copy-start(bf16[2048,128]{0,1:T(8,128)(2,1)} %copy-done.2) | copy-start | bytes 1572868
  95.6 83.7 %all-to-all-start.1 = ((bf16[16,64,128]{2,1,0:T(8,128)(2,1)}), bf16[16,64,128]{2,1,0:T(8,128)(2,1)}, u32[]{:S(2)}, u32[]{:S(2)}) async-start(bf16[16,64,128]{2,1,0:T(8,128)(2,1)} %add_convert_fusion), calls=%async_computation.1 | async-start | bytes 524288 | tf_op jit(solution)/shard_map/all_to_all | solution.py:103
  102.0 25.2 %all-reduce.9.cloned.1.call-start = ((), (), s32[]{:S(2)}) async-start(), calls=%async_computation.3 | async-start | bytes 917504 | tf_op jit(solution)/shard_map/psum | solution.py:113
  102.8 24.5 %copy-start.7 = (bf16[512,256]{0,1:T(8,128)(2,1)S(1)}, bf16[512,256]{0,1:T(8,128)(2,1)}, u32[]{:S(2)}) copy-start(bf16[512,256]{0,1:T(8,128)(2,1)} %copy-done.6) | copy-start | bytes 786436
  102.8 139.3 %all-reduce.7.cloned.1.call-start = ((), (), s32[]{:S(2)}) async-start(), calls=%async_computation.2 | async-start | bytes 917504 | tf_op jit(solution)/shard_map/psum | solution.py:112
  104.0 23.3 %copy-start.5 = (f32[1,2048,128]{1,2,0:T(8,128)S(1)}, f32[1,2048,128]{1,2,0:T(8,128)}, u32[]{:S(2)}) copy-start(f32[1,2048,128]{1,2,0:T(8,128)} %add_bitcast_fusion) | copy-start | bytes 3145732
  129.3 11.6 %copy-start.37 = (f32[128]{0:T(128)S(1)}, f32[128]{0:T(128)}, u32[]{:S(2)}) copy-start(f32[128]{0:T(128)} %get-tuple-element.26) | copy-start | bytes 1540
  129.3 11.6 %copy-start.38 = (f32[128]{0:T(128)S(1)}, f32[128]{0:T(128)}, u32[]{:S(2)}) copy-start(f32[128]{0:T(128)} %get-tuple-element.24) | copy-start | bytes 1540
  185.0 63.2 %copy-start = (f32[512,128]{1,0:T(8,128)}, f32[512,128]{1,0:T(8,128)S(1)}, u32[]{:S(2)}) copy-start(f32[512,128]{1,0:T(8,128)S(1)} %scatter_custom_fusion.6) | copy-start | bytes 786436
  (16 other events, 14.4 us)
Sparse Core Ops, SparseCore 0:
  106.0 21.2 all-reduce.8
  132.7 109.2 all-reduce.6
